TPU v7x, 256 devices: a whole 4x4x8 slice. The times are simulated.
256 devices in a mesh: gx: 16 (over z, y_lo), gy: 4 (over x), gz: 4 (over y_hi, core).
Axes of the slice: x: 4, y: 4 (y_hi: 2, y_lo: 2; y = y_hi * 2 + y_lo), z: 8, core: 2. Of those that a mesh axis runs over, the one named last changes fastest.
Arguments:
- positions: float32 [3, 32, 8, 8, 128], P(None, 'gx', 'gy', 'gz'), may hold values from 0 to 1
- velocities: float32 [3, 32, 8, 8, 128], P(None, 'gx', 'gy', 'gz'), may hold values from -1.8 to 1.8
- pressure_prev: float32 [32, 8, 8, 128], P('gx', 'gy', 'gz'), may hold values from 0 to 0.5
- counts: int32 [32, 8, 8], P('gx', 'gy', 'gz'), may hold values from 1 to 128, as said below
- out_positions: float32 [3, 16, 4, 4, 128], P(None, 'gx', 'gy', 'gz'), may hold values from 0 to 1
- out_velocities: float32 [3, 16, 4, 4, 128], P(None, 'gx', 'gy', 'gz'), may hold values from -1.8 to 1.8
- out_dir: int32 [16, 4, 4, 128], P('gx', 'gy', 'gz'), may hold values from 0 to 5, as said below
- out_cell: int32 [16, 4, 4, 128], P('gx', 'gy', 'gz'), may hold values from 0 to 7, as said below
- out_count: int32 [16, 4, 4], P('gx', 'gy', 'gz'), may hold values from 1 to 128, as said below
Outputs:
- pressure: float32 [32, 8, 8, 128], P('gx', 'gy', 'gz')
- velocity_new: float32 [3, 32, 8, 8, 128], P(None, 'gx', 'gy', 'gz')
- density_error: float32 [2], replicated
Inputs may be any that keep to these rules, and one draw needn't show every extreme that they name: `counts`: each cell's count plus the live outbox slots bound for it is at most 128. `out_dir`: 0 +x, 1 -x, 2 +y, 3 -y, 4 +z, 5 -z. `out_cell`: local index in the receiving block, of a cell on the face through which the particle enters. `out_count`: the live slots are the first ones.
All inputs are finite; a program needn't handle non-finite values.
Results may differ from a plain program's by a relative error of at most 0.0003.
Values sent between devices are 32-bit elements; how exact they have to be, the bound alone decides.
No kernel may reach another device: no remote copies, remote signals or barrier semaphores. Data moves between devices by JAX's collectives and lax.ppermute only.
A program may use at most 64 MiB of HBM per device.

v0:
```python
import jax
import jax.numpy as jnp
from jax import lax
from jax.sharding import Mesh
from jax.sharding import PartitionSpec as P

ITERS = 2
GX = ("gx_0", "gx_1")
GZ = ("gz_0", "gz_1")
GX_GY_GZ = ("gx_0", "gx_1", "gy", "gz_0", "gz_1")
kernel_var = 0.25
time_step = 2.0
particle_mass = 1.0 / 45.0
rest_density = 1.0
relaxation = 0.5
floor_value = 0.1
gravity = 0.1


def passed_along(x, axis, by):
    size = lax.axis_size(axis)
    pairs = [(i, i + by) for i in range(size) if 0 <= i + by < size]
    return lax.ppermute(x, axis, pairs)


def with_halo(block, sides, width):
    for axis, dim in sides:
        count = lax.axis_size(axis)
        forward = [(i, i + 1) for i in range(count - 1)]
        backward = [(target, source) for source, target in forward]
        low = lax.ppermute(
            lax.slice_in_dim(block, block.shape[dim] - width, None, axis=dim), axis, forward
        )
        high = lax.ppermute(lax.slice_in_dim(block, 0, width, axis=dim), axis, backward)
        block = jnp.concatenate([low, block, high], axis=dim)
    return block


def one_axis_at_a_time(x, axes):
    for axis in axes:
        x = lax.psum(x, axis)
    return x


def stencil_offsets():
    return [(a, b, c) for a in (-1, 0, 1) for b in (-1, 0, 1) for c in (-1, 0, 1)]


def window(padded, offset, extent):
    return padded[
        :,
        1 + offset[0] : 1 + offset[0] + extent[0],
        1 + offset[1] : 1 + offset[1] + extent[1],
        1 + offset[2] : 1 + offset[2] + extent[2],
        :,
    ]


def geometry(center_pos, other_pos, offset):
    deltas = [
        center_pos[k][..., :, None] - other_pos[k][..., None, :] - float(offset[k])
        for k in range(3)
    ]
    distance = deltas[0] * deltas[0] + deltas[1] * deltas[1] + deltas[2] * deltas[2]
    kernel = jnp.exp(-distance / kernel_var)
    factor = -2.0 / kernel_var * kernel
    return (kernel, [factor * d for d in deltas])


def setup_pass(center_pos, center_vel, near_pos, near_vel, near_mass):
    extent = center_pos.shape[1:4]
    zeros = jnp.zeros(center_pos.shape[1:], jnp.float32)
    density, divergence, grad_square = (zeros, zeros, zeros)
    grad_sum = [zeros, zeros, zeros]
    for offset in stencil_offsets():
        other_pos = window(near_pos, offset, extent)
        other_vel = window(near_vel, offset, extent)
        masses = window(near_mass, offset, extent)[0][..., None, :]
        kernel, grads = geometry(center_pos, other_pos, offset)
        density = density + jnp.sum(masses * kernel, -1)
        closing = sum(
            (
                (center_vel[k][..., :, None] - other_vel[k][..., None, :]) * grads[k]
                for k in range(3)
            )
        )
        divergence = divergence + jnp.sum(masses * closing, -1)
        grad_sum = [grad_sum[k] + jnp.sum(masses * grads[k], -1) for k in range(3)]
        grad_square = grad_square + jnp.sum(
            masses * (grads[0] * grads[0] + grads[1] * grads[1] + grads[2] * grads[2]), -1
        )
    return jnp.stack([density, divergence, grad_sum[0], grad_sum[1], grad_sum[2], grad_square])


def accel_pass(center_pos, center_scaled, near_pos, near_mass, near_scaled):
    extent = center_pos.shape[1:4]
    zeros = jnp.zeros(center_pos.shape[1:], jnp.float32)
    totals = [zeros, zeros, zeros]
    for offset in stencil_offsets():
        other_pos = window(near_pos, offset, extent)
        masses = window(near_mass, offset, extent)[0][..., None, :]
        others = window(near_scaled, offset, extent)[0][..., None, :]
        kernel, grads = geometry(center_pos, other_pos, offset)
        factor = masses * (center_scaled[0][..., :, None] + others)
        totals = [totals[k] + jnp.sum(factor * grads[k], -1) for k in range(3)]
    return -jnp.stack(totals)


def apply_pass(center_pos, center_acc, near_pos, near_mass, near_acc):
    extent = center_pos.shape[1:4]
    total = jnp.zeros(center_pos.shape[1:], jnp.float32)
    for offset in stencil_offsets():
        other_pos = window(near_pos, offset, extent)
        masses = window(near_mass, offset, extent)[0][..., None, :]
        other_acc = window(near_acc, offset, extent)
        kernel, grads = geometry(center_pos, other_pos, offset)
        closing = sum(
            (
                (center_acc[k][..., :, None] - other_acc[k][..., None, :]) * grads[k]
                for k in range(3)
            )
        )
        total = total + jnp.sum(masses * closing, -1)
    return (time_step * time_step * total)[None]


def payloads(out_positions, out_velocities, out_dir, out_cell, out_count):
    migrants = out_dir.shape[-1]
    living = jnp.arange(migrants, dtype=jnp.int32) < out_count[..., None]
    cargo = jnp.concatenate([out_positions, out_velocities], 0)
    result = []
    for d in range(6):
        tagged = jnp.where(living & (out_dir == d), out_cell + 1, 0).astype(jnp.float32)
        result.append(jnp.concatenate([cargo, tagged[None]], 0))
    return result


def insert(particle_state, counts, arrivals):
    cell_total = counts.size
    slots = particle_state.shape[-1]
    flat_state = particle_state.reshape(6, cell_total * slots)
    filled = counts.reshape(cell_total)
    tagged = arrivals[6].astype(jnp.int32) - 1
    onehot = (tagged[:, None] == jnp.arange(cell_total, dtype=jnp.int32)[None, :]).astype(jnp.int32)
    ranked = jnp.cumsum(onehot, 0, dtype=jnp.int32) - onehot
    start = jnp.sum(onehot * filled[None, :], 1, dtype=jnp.int32)
    within = jnp.sum(onehot * ranked, 1, dtype=jnp.int32)
    target = jnp.where(tagged >= 0, tagged * slots + start + within, cell_total * slots)
    placed = jax.ops.segment_sum(arrivals[:6].T, target, num_segments=cell_total * slots + 1)[
        : cell_total * slots
    ].T
    slot_index = jnp.arange(slots, dtype=jnp.int32)
    kept = (slot_index[None, :] < filled[:, None]).reshape(cell_total * slots)
    merged = jnp.where(kept[None, :], flat_state, placed)
    grown = filled + jnp.sum(onehot, 0, dtype=jnp.int32)
    return (merged.reshape(particle_state.shape), grown.reshape(counts.shape))


def on_device(
    positions,
    velocities,
    pressure_prev,
    counts,
    out_positions,
    out_velocities,
    out_dir,
    out_cell,
    out_count,
):
    cargo = payloads(out_positions, out_velocities, out_dir, out_cell, out_count)
    received = []
    for offset_sign, heading in ((1, 0), (-1, 1)):
        received.append(passed_along(cargo[heading], GX, offset_sign))
    for offset_sign, heading in ((1, 2), (-1, 3)):
        received.append(passed_along(cargo[heading], "gy", offset_sign))
    for offset_sign, heading in ((1, 4), (-1, 5)):
        received.append(passed_along(cargo[heading], GZ, offset_sign))
    arrivals = jnp.concatenate(received, -1).reshape(7, -1)
    particle_state, new_counts = insert(
        jnp.concatenate([positions, velocities], 0), counts, arrivals
    )
    slot_index = jnp.arange(positions.shape[-1], dtype=jnp.int32)
    occupied = slot_index < new_counts[..., None]
    was_there = slot_index < counts[..., None]
    masses = jnp.where(occupied, particle_mass, 0.0).astype(jnp.float32)[None]
    local_state = jnp.concatenate([particle_state, masses], 0)
    local_pos = particle_state[0:3]
    local_vel = particle_state[3:6]
    near_state = with_halo(local_state, ((GX, 1), ("gy", 2), (GZ, 3)), 1)
    near_pos = near_state[0:3]
    near_mass = near_state[6:7]
    summary = setup_pass(local_pos, local_vel, near_pos, near_state[3:6], near_mass)
    density, divergence, grad_square = (summary[0], summary[1], summary[5])
    safe = jnp.where(occupied, density, 1.0)
    source = jnp.where(occupied, rest_density - (density + time_step * divergence), 0.0)
    grad_norm = summary[2] * summary[2] + summary[3] * summary[3] + summary[4] * summary[4]
    diagonal = jnp.maximum(
        time_step * time_step * (grad_norm + masses[0] * grad_square) / (safe * safe), floor_value
    )
    pressure = jnp.where(was_there, pressure_prev, 0.0)
    total_slots = (
        positions.shape[1]
        * positions.shape[2]
        * positions.shape[3]
        * positions.shape[4]
        * lax.axis_size(GX)
        * lax.axis_size("gy")
        * lax.axis_size(GZ)
    )
    errors = []
    for _ in range(ITERS):
        scaled = jnp.where(occupied, pressure / (safe * safe), 0.0)[None]
        scaled_near = with_halo(scaled, ((GX, 1), ("gy", 2), (GZ, 3)), 1)
        accel_local = accel_pass(local_pos, scaled, near_pos, near_mass, scaled_near)
        accel_near = with_halo(accel_local, ((GX, 1), ("gy", 2), (GZ, 3)), 1)
        applied = apply_pass(local_pos, accel_local, near_pos, near_mass, accel_near)[0]
        residual = jnp.where(occupied, source - applied, 0.0)
        share_error = jnp.sum(jnp.abs(residual)) / total_slots
        errors.append(share_error)
        pressure = jnp.where(
            occupied, jnp.maximum(pressure + relaxation * (applied - source) / diagonal, 0.0), 0.0
        )
    density_error = one_axis_at_a_time(jnp.stack(errors), GX_GY_GZ)
    scaled = jnp.where(occupied, pressure / (safe * safe), 0.0)[None]
    scaled_near = with_halo(scaled, ((GX, 1), ("gy", 2), (GZ, 3)), 1)
    accel = accel_pass(local_pos, scaled, near_pos, near_mass, scaled_near)
    pulled = accel + jnp.array([0.0, 0.0, -gravity], jnp.float32)[:, None, None, None, None]
    velocity_new = jnp.where(occupied[None], local_vel + time_step * pulled, 0.0)
    return (pressure, velocity_new, density_error)


def solution(mesh):
    torus = Mesh(
        mesh.devices.reshape(8, 2, mesh.shape["gy"], 2, 2), ("gx_0", "gx_1", "gy", "gz_0", "gz_1")
    )
    in_specs = (
        P(None, GX, "gy", GZ, None),
        P(None, GX, "gy", GZ, None),
        P(GX, "gy", GZ, None),
        P(GX, "gy", GZ),
        P(None, GX, "gy", GZ, None),
        P(None, GX, "gy", GZ, None),
        P(GX, "gy", GZ, None),
        P(GX, "gy", GZ, None),
        P(GX, "gy", GZ),
    )
    out_specs = (P(GX, "gy", GZ, None), P(None, GX, "gy", GZ, None), P())
    return jax.shard_map(
        on_device, mesh=torus, in_specs=in_specs, out_specs=out_specs, check_vma=False
    )
```

profile of v0, /device:TPU:24, one launch (start us, length us, event | category | flops | bytes accessed | tf_op | source)
XLA Modules:
  0.0 421.0 jit_solution(3058559179890980939)
XLA Ops:
  8.5 4.5 %collective-permute-start.2 = (f32[7,1,1,1,128]{4,3,2,1,0:T(1,128)S(1)}, f32[7,1,1,1,128]{4,3,2,1,0:T(1,128)S(1)}, u32[]{:S(2)}, u32[]{:S(2)}) collective-permute-start(f32[7,1,1,1,128]{4,3,2,1,0:T(1,128)S(1)} %get-tuple-element.1061), channel_id=1, source_target_pairs={{0,4},{4,8},{8,12},{1,5},{5,9},{9,13},{2,6},{6,10},{10,14},{3,7},{... | collective-permute-start | bytes 10760 | tf_op jit(solution)/shard_map/ppermute | solution.py:23
  13.1 3.8 collective-permute-start
  20.5 4.5 %collective-permute-done.1 = f32[7,1,1,1,128]{4,3,2,1,0:T(1,128)S(1)} collective-permute-done((f32[7,1,1,1,128]{4,3,2,1,0:T(1,128)S(1)}, f32[7,1,1,1,128]{4,3,2,1,0:T(1,128)S(1)}, u32[]{:S(2)}, u32[]{:S(2)}) %collective-permute-start.1) | collective-permute-done | bytes 3616 | tf_op jit(solution)/shard_map/ppermute | solution.py:23
  27.9 6.9 %scatter_custom_fusion = f32[1025,6]{1,0:T(8,128)S(1)} fusion(s32[768]{0:T(1024)S(1)} %fusion.171, f32[6,1,1,1,768]{0,4,1,2,3:T(8,128)S(1)} %copy.31, f32[]{:T(128)} %constant.125.clone.1), kind=kCustom, calls=%fused_computation.810 | custom fusion | flops 4608 | bytes 417820 | tf_op jit(solution)/shard_map/scatter-add | solution.py:149
  35.2 3.8 collective-permute-start.6
  42.7 2.9 collective-permute-done.7
  45.6 3.2 collective-permute-start.8
  50.4 4.2 %collective-permute-done.9 = f32[7,4,1,2,128]{4,3,2,1,0:T(2,128)S(1)} collective-permute-done((f32[7,4,1,2,128]{4,3,2,1,0:T(2,128)S(1)}, f32[7,4,1,2,128]{4,3,2,1,0:T(2,128)S(1)}, u32[]{:S(2)}, u32[]{:S(2)}) %collective-permute-start.9) | collective-permute-done | bytes 28704 | tf_op jit(solution)/shard_map/ppermute | solution.py:34
  59.7 4.0 collective-permute-done.10
  79.1 3.1 collective-permute-start.13
  82.2 3.2 collective-permute-done.13
  85.5 3.3 collective-permute-start.14
  96.3 5.3 %collective-permute-start.17 = (f32[1,4,4,1,128]{4,3,2,1,0:T(1,128)S(1)}, f32[1,4,4,1,128]{4,3,2,1,0:T(1,128)S(1)}, u32[]{:S(2)}, u32[]{:S(2)}) collective-permute-start(f32[1,4,4,1,128]{4,3,2,1,0:T(1,128)S(1)} %get-tuple-element.1000), channel_id=1, source_target_pairs={{1,0},{2,1},{3,2},{5,4},{6,5},{7,6},{9,8},{10,9},{11,10},{13,12},{... | collective-permute-start | bytes 24584 | tf_op jit(solution)/shard_map/ppermute | solution.py:34
  144.8 3.9 collective-permute-start.18
  150.7 4.5 %collective-permute-done.19 = f32[3,1,2,2,128]{4,3,2,1,0:T(2,128)S(1)} collective-permute-done((f32[3,1,2,2,128]{4,3,2,1,0:T(2,128)S(1)}, f32[3,1,2,2,128]{4,3,2,1,0:T(2,128)S(1)}, u32[]{:S(2)}, u32[]{:S(2)}) %collective-permute-start.19) | collective-permute-done | bytes 6176 | tf_op jit(solution)/shard_map/ppermute | solution.py:34
  156.5 4.5 %collective-permute-start.20 = (f32[3,4,1,2,128]{4,3,2,1,0:T(2,128)S(1)}, f32[3,4,1,2,128]{4,3,2,1,0:T(2,128)S(1)}, u32[]{:S(2)}, u32[]{:S(2)}) collective-permute-start(f32[3,4,1,2,128]{4,3,2,1,0:T(2,128)S(1)} %get-tuple-element.976), channel_id=1, source_target_pairs={{0,4},{4,8},{8,12},{1,5},{5,9},{9,13},{2,6},{6,10},{10,14},{3,7},{... | collective-permute-start | bytes 36872 | tf_op jit(solution)/shard_map/ppermute | solution.py:31
  176.7 3.3 multiply_reduce_fusion.349
  215.3 3.2 collective-permute-start.24
  221.2 4.9 %collective-permute-done.25 = f32[1,1,2,2,128]{4,3,2,1,0:T(2,128)S(1)} collective-permute-done((f32[1,1,2,2,128]{4,3,2,1,0:T(2,128)S(1)}, f32[1,1,2,2,128]{4,3,2,1,0:T(2,128)S(1)}, u32[]{:S(2)}, u32[]{:S(2)}) %collective-permute-start.25) | collective-permute-done | bytes 2080 | tf_op jit(solution)/shard_map/ppermute | solution.py:34
  226.1 3.9 collective-permute-start.26
  231.3 4.2 collective-permute-done.27
  239.9 4.2 collective-permute-done.28
  244.2 3.1 multiply_reduce_fusion.175
  250.2 2.9 multiply_reduce_fusion.164
  253.1 2.9 multiply_reduce_fusion.167
  258.9 2.9 multiply_reduce_fusion.179
  261.8 2.9 multiply_reduce_fusion.182
  267.6 2.9 multiply_reduce_fusion.176
  270.7 3.9 collective-permute-start.30
  276.6 4.8 %collective-permute-done.31 = f32[3,1,2,2,128]{4,3,2,1,0:T(2,128)S(1)} collective-permute-done((f32[3,1,2,2,128]{4,3,2,1,0:T(2,128)S(1)}, f32[3,1,2,2,128]{4,3,2,1,0:T(2,128)S(1)}, u32[]{:S(2)}, u32[]{:S(2)}) %collective-permute-start.31) | collective-permute-done | bytes 6176 | tf_op jit(solution)/shard_map/ppermute | solution.py:34
  291.2 5.1 %collective-permute-start.35 = (f32[3,4,4,1,128]{4,3,2,1,0:T(1,128)S(1)}, f32[3,4,4,1,128]{4,3,2,1,0:T(1,128)S(1)}, u32[]{:S(2)}, u32[]{:S(2)}) collective-permute-start(f32[3,4,4,1,128]{4,3,2,1,0:T(1,128)S(1)} %get-tuple-element.858), channel_id=1, source_target_pairs={{1,0},{2,1},{3,2},{5,4},{6,5},{7,6},{9,8},{10,9},{11,10},{13,12},{... | collective-permute-start | bytes 73736 | tf_op jit(solution)/shard_map/ppermute | solution.py:34
  328.5 17.9 %psum.35 = f32[2]{0:T(128)S(1)} all-reduce(f32[2]{0:T(128)S(1)} %pad_maximum_fusion.47), channel_id=1, replica_groups=mesh['gx_0'=8,'gx_1'=2,'gy'=4,'gz_0'=2,'gz_1'=2] {'gx_0'}, use_global_device_ids=true, to_apply=%region_467.468 | all-reduce | flops 2 | bytes 16 | tf_op jit(solution)/shard_map/psum | solution.py:41
  346.3 4.9 %psum.36 = f32[2]{0:T(128)S(1)} all-reduce(f32[2]{0:T(128)S(1)} %psum.35), channel_id=1, replica_groups=mesh['gx_0'=8,'gx_1'=2,'gy'=4,'gz_0'=2,'gz_1'=2] {'gx_1'}, use_global_device_ids=true, to_apply=%region_468.469 | all-reduce | flops 2 | bytes 16 | tf_op jit(solution)/shard_map/psum | solution.py:41
  353.8 3.9 collective-permute-start.37
  357.8 8.5 %psum.37 = f32[2]{0:T(128)S(1)} all-reduce(f32[2]{0:T(128)S(1)} %psum.36), channel_id=1, replica_groups=mesh['gx_0'=8,'gx_1'=2,'gy'=4,'gz_0'=2,'gz_1'=2] {'gy'}, use_global_device_ids=true, to_apply=%region_469.470 | all-reduce | flops 2 | bytes 16 | tf_op jit(solution)/shard_map/psum | solution.py:41
  366.5 6.4 %psum.38 = f32[2]{0:T(128)S(1)} all-reduce(f32[2]{0:T(128)S(1)} %psum.37), channel_id=1, replica_groups=mesh['gx_0'=8,'gx_1'=2,'gy'=4,'gz_0'=2,'gz_1'=2] {'gz_0'}, use_global_device_ids=true, to_apply=%region_470.471 | all-reduce | flops 2 | bytes 16 | tf_op jit(solution)/shard_map/psum | solution.py:41
  373.2 3.0 psum.39
  376.1 3.1 collective-permute-start.38
  380.6 4.2 collective-permute-done.39
  389.2 4.0 collective-permute-done.40
  393.3 2.9 multiply_reduce_fusion.67
  399.1 2.9 multiply_reduce_fusion.74
  402.0 2.9 multiply_reduce_fusion.71
  404.9 2.9 multiply_reduce_fusion.68
  407.8 2.9 multiply_reduce_fusion.62
  410.7 2.9 multiply_reduce_fusion.59
  413.6 2.9 multiply_reduce_fusion.79
  416.5 2.9 multiply_reduce_fusion.56
  (298 shorter events, 216.4 us)
Async XLA Ops:
  1.9 0.7 copy-start.5
  2.0 0.7 copy-start.4
  2.7 22.4 %collective-permute-start.5 = (f32[7,1,1,1,128]{4,3,2,1,0:T(1,128)S(1)}, f32[7,1,1,1,128]{4,3,2,1,0:T(1,128)S(1)}, u32[]{:S(2)}, u32[]{:S(2)}) collective-permute-start(f32[7,1,1,1,128]{4,3,2,1,0:T(1,128)S(1)} %get-tuple-element.569), channel_id=1, source_target_pairs={{1,0},{2,1},{3,2},{5,4},{6,5},{7,6},{9,8},{10,9},{11,10},{13,12},{... | collective-permute-start | bytes 10760 | tf_op jit(solution)/shard_map/ppermute | solution.py:23
  5.2 11.8 %copy-start.2 = (f32[3,2,2,2,128]{4,3,2,1,0:T(2,128)S(1)}, f32[3,2,2,2,128]{4,3,2,1,0:T(2,128)}, u32[]{:S(2)}) copy-start(f32[3,2,2,2,128]{4,3,2,1,0:T(2,128)} %param.11) | copy-start | bytes 36868
  5.3 11.8 %copy-start.3 = (f32[3,2,2,2,128]{4,3,2,1,0:T(2,128)S(1)}, f32[3,2,2,2,128]{4,3,2,1,0:T(2,128)}, u32[]{:S(2)}) copy-start(f32[3,2,2,2,128]{4,3,2,1,0:T(2,128)} %param.10) | copy-start | bytes 36868
  5.3 19.7 %collective-permute-start.4 = (f32[7,1,1,1,128]{4,3,2,1,0:T(1,128)S(1)}, f32[7,1,1,1,128]{4,3,2,1,0:T(1,128)S(1)}, u32[]{:S(2)}, u32[]{:S(2)}) collective-permute-start(f32[7,1,1,1,128]{4,3,2,1,0:T(1,128)S(1)} %get-tuple-element.1059), channel_id=1, source_target_pairs={{0,1},{1,2},{2,3},{4,5},{5,6},{6,7},{8,9},{9,10},{10,11},{12,13},{... | collective-permute-start | bytes 10760 | tf_op jit(solution)/shard_map/ppermute | solution.py:23
  7.2 9.7 %copy-start = (s32[2,2,2]{2,1,0:T(2,128)S(1)}, s32[2,2,2]{2,1,0:T(2,128)}, u32[]{:S(2)}) copy-start(s32[2,2,2]{2,1,0:T(2,128)} %param.13) | copy-start | bytes 100
  7.2 17.8 %collective-permute-start.3 = (f32[7,1,1,1,128]{4,3,2,1,0:T(1,128)S(1)}, f32[7,1,1,1,128]{4,3,2,1,0:T(1,128)S(1)}, u32[]{:S(2)}, u32[]{:S(2)}) collective-permute-start(f32[7,1,1,1,128]{4,3,2,1,0:T(1,128)S(1)} %get-tuple-element.1060), channel_id=1, source_target_pairs={{4,0},{8,4},{12,8},{5,1},{9,5},{13,9},{6,2},{10,6},{14,10},{7,3},{... | collective-permute-start | bytes 10760 | tf_op jit(solution)/shard_map/ppermute | solution.py:23
  8.5 16.4 %collective-permute-start.2 = (f32[7,1,1,1,128]{4,3,2,1,0:T(1,128)S(1)}, f32[7,1,1,1,128]{4,3,2,1,0:T(1,128)S(1)}, u32[]{:S(2)}, u32[]{:S(2)}) collective-permute-start(f32[7,1,1,1,128]{4,3,2,1,0:T(1,128)S(1)} %get-tuple-element.1061), channel_id=1, source_target_pairs={{0,4},{4,8},{8,12},{1,5},{5,9},{9,13},{2,6},{6,10},{10,14},{3,7},{... | collective-permute-start | bytes 10760 | tf_op jit(solution)/shard_map/ppermute | solution.py:23
  13.1 5.5 %collective-permute-start = (f32[7,1,1,1,128]{4,3,2,1,0:T(1,128)S(1)}, f32[7,1,1,1,128]{4,3,2,1,0:T(1,128)S(1)}, u32[]{:S(2)}, u32[]{:S(2)}) collective-permute-start(f32[7,1,1,1,128]{4,3,2,1,0:T(1,128)S(1)} %get-tuple-element.1063), channel_id=1, source_target_pairs={{0,16},{16,32},{32,48},{48,64},{64,80},{80,96},{96,112},{112,128},... | collective-permute-start | bytes 10760 | tf_op jit(solution)/shard_map/ppermute | solution.py:23
  18.6 6.4 %collective-permute-start.1 = (f32[7,1,1,1,128]{4,3,2,1,0:T(1,128)S(1)}, f32[7,1,1,1,128]{4,3,2,1,0:T(1,128)S(1)}, u32[]{:S(2)}, u32[]{:S(2)}) collective-permute-start(f32[7,1,1,1,128]{4,3,2,1,0:T(1,128)S(1)} %get-tuple-element.1062), channel_id=1, source_target_pairs={{16,0},{32,16},{48,32},{64,48},{80,64},{96,80},{112,96},{128,112},... | collective-permute-start | bytes 10760 | tf_op jit(solution)/shard_map/ppermute | solution.py:23
  35.2 7.4 %collective-permute-start.6 = (f32[7,1,2,2,128]{4,3,2,1,0:T(2,128)S(1)}, f32[7,1,2,2,128]{4,3,2,1,0:T(2,128)S(1)}, u32[]{:S(2)}, u32[]{:S(2)}) collective-permute-start(f32[7,1,2,2,128]{4,3,2,1,0:T(2,128)S(1)} %get-tuple-element.967), channel_id=1, source_target_pairs={{0,16},{16,32},{32,48},{48,64},{64,80},{80,96},{96,112},{112,128},... | collective-permute-start | bytes 43016 | tf_op jit(solution)/shard_map/ppermute | solution.py:31
  39.1 6.5 %collective-permute-start.7 = (f32[7,1,2,2,128]{4,3,2,1,0:T(2,128)S(1)}, f32[7,1,2,2,128]{4,3,2,1,0:T(2,128)S(1)}, u32[]{:S(2)}, u32[]{:S(2)}) collective-permute-start(f32[7,1,2,2,128]{4,3,2,1,0:T(2,128)S(1)} %get-tuple-element.968), channel_id=1, source_target_pairs={{16,0},{32,16},{48,32},{64,48},{80,64},{96,80},{112,96},{128,112},... | collective-permute-start | bytes 43016 | tf_op jit(solution)/shard_map/ppermute | solution.py:34
  45.6 4.8 %collective-permute-start.8 = (f32[7,4,1,2,128]{4,3,2,1,0:T(2,128)S(1)}, f32[7,4,1,2,128]{4,3,2,1,0:T(2,128)S(1)}, u32[]{:S(2)}, u32[]{:S(2)}) collective-permute-start(f32[7,4,1,2,128]{4,3,2,1,0:T(2,128)S(1)} %get-tuple-element.853), channel_id=1, source_target_pairs={{0,4},{4,8},{8,12},{1,5},{5,9},{9,13},{2,6},{6,10},{10,14},{3,7},{... | collective-permute-start | bytes 86024 | tf_op jit(solution)/shard_map/ppermute | solution.py:31
  48.9 5.8 %collective-permute-start.9 = (f32[7,4,1,2,128]{4,3,2,1,0:T(2,128)S(1)}, f32[7,4,1,2,128]{4,3,2,1,0:T(2,128)S(1)}, u32[]{:S(2)}, u32[]{:S(2)}) collective-permute-start(f32[7,4,1,2,128]{4,3,2,1,0:T(2,128)S(1)} %get-tuple-element.854), channel_id=1, source_target_pairs={{4,0},{8,4},{12,8},{5,1},{9,5},{13,9},{6,2},{10,6},{14,10},{7,3},{... | collective-permute-start | bytes 86024 | tf_op jit(solution)/shard_map/ppermute | solution.py:34
  54.8 5.0 %collective-permute-start.11 = (f32[7,4,4,1,128]{4,3,2,1,0:T(1,128)S(1)}, f32[7,4,4,1,128]{4,3,2,1,0:T(1,128)S(1)}, u32[]{:S(2)}, u32[]{:S(2)}) collective-permute-start(f32[7,4,4,1,128]{4,3,2,1,0:T(1,128)S(1)} %get-tuple-element.699), channel_id=1, source_target_pairs={{1,0},{2,1},{3,2},{5,4},{6,5},{7,6},{9,8},{10,9},{11,10},{13,12},{... | collective-permute-start | bytes 172040 | tf_op jit(solution)/shard_map/ppermute | solution.py:34
  56.7 7.0 %collective-permute-start.10 = (f32[7,4,4,1,128]{4,3,2,1,0:T(1,128)S(1)}, f32[7,4,4,1,128]{4,3,2,1,0:T(1,128)S(1)}, u32[]{:S(2)}, u32[]{:S(2)}) collective-permute-start(f32[7,4,4,1,128]{4,3,2,1,0:T(1,128)S(1)} %get-tuple-element.700), channel_id=1, source_target_pairs={{0,1},{1,2},{2,3},{4,5},{5,6},{6,7},{8,9},{9,10},{10,11},{12,13},{... | collective-permute-start | bytes 172040 | tf_op jit(solution)/shard_map/ppermute | solution.py:31
  75.5 0.7 copy-start.1
  76.3 5.9 %collective-permute-start.12 = (f32[1,1,2,2,128]{4,3,2,1,0:T(2,128)S(1)}, f32[1,1,2,2,128]{4,3,2,1,0:T(2,128)S(1)}, u32[]{:S(2)}, u32[]{:S(2)}) collective-permute-start(f32[1,1,2,2,128]{4,3,2,1,0:T(2,128)S(1)} %get-tuple-element.1057), channel_id=1, source_target_pairs={{0,16},{16,32},{32,48},{48,64},{64,80},{80,96},{96,112},{112,128},... | collective-permute-start | bytes 6152 | tf_op jit(solution)/shard_map/ppermute | solution.py:31
  79.1 6.4 %collective-permute-start.13 = (f32[1,1,2,2,128]{4,3,2,1,0:T(2,128)S(1)}, f32[1,1,2,2,128]{4,3,2,1,0:T(2,128)S(1)}, u32[]{:S(2)}, u32[]{:S(2)}) collective-permute-start(f32[1,1,2,2,128]{4,3,2,1,0:T(2,128)S(1)} %get-tuple-element.1058), channel_id=1, source_target_pairs={{16,0},{32,16},{48,32},{64,48},{80,64},{96,80},{112,96},{128,112},... | collective-permute-start | bytes 6152 | tf_op jit(solution)/shard_map/ppermute | solution.py:34
  85.5 8.2 %collective-permute-start.14 = (f32[1,4,1,2,128]{4,3,2,1,0:T(2,128)S(1)}, f32[1,4,1,2,128]{4,3,2,1,0:T(2,128)S(1)}, u32[]{:S(2)}, u32[]{:S(2)}) collective-permute-start(f32[1,4,1,2,128]{4,3,2,1,0:T(2,128)S(1)} %get-tuple-element.1045), channel_id=1, source_target_pairs={{0,4},{4,8},{8,12},{1,5},{5,9},{9,13},{2,6},{6,10},{10,14},{3,7},{... | collective-permute-start | bytes 12296 | tf_op jit(solution)/shard_map/ppermute | solution.py:31
  88.8 5.5 %collective-permute-start.15 = (f32[1,4,1,2,128]{4,3,2,1,0:T(2,128)S(1)}, f32[1,4,1,2,128]{4,3,2,1,0:T(2,128)S(1)}, u32[]{:S(2)}, u32[]{:S(2)}) collective-permute-start(f32[1,4,1,2,128]{4,3,2,1,0:T(2,128)S(1)} %get-tuple-element.1046), channel_id=1, source_target_pairs={{4,0},{8,4},{12,8},{5,1},{9,5},{13,9},{6,2},{10,6},{14,10},{7,3},{... | collective-permute-start | bytes 12296 | tf_op jit(solution)/shard_map/ppermute | solution.py:34
  94.3 17.9 %collective-permute-start.16 = (f32[1,4,4,1,128]{4,3,2,1,0:T(1,128)S(1)}, f32[1,4,4,1,128]{4,3,2,1,0:T(1,128)S(1)}, u32[]{:S(2)}, u32[]{:S(2)}) collective-permute-start(f32[1,4,4,1,128]{4,3,2,1,0:T(1,128)S(1)} %get-tuple-element.999), channel_id=1, source_target_pairs={{0,1},{1,2},{2,3},{4,5},{5,6},{6,7},{8,9},{9,10},{10,11},{12,13},{... | collective-permute-start | bytes 24584 | tf_op jit(solution)/shard_map/ppermute | solution.py:31
  96.3 16.0 %collective-permute-start.17 = (f32[1,4,4,1,128]{4,3,2,1,0:T(1,128)S(1)}, f32[1,4,4,1,128]{4,3,2,1,0:T(1,128)S(1)}, u32[]{:S(2)}, u32[]{:S(2)}) collective-permute-start(f32[1,4,4,1,128]{4,3,2,1,0:T(1,128)S(1)} %get-tuple-element.1000), channel_id=1, source_target_pairs={{1,0},{2,1},{3,2},{5,4},{6,5},{7,6},{9,8},{10,9},{11,10},{13,12},{... | collective-permute-start | bytes 24584 | tf_op jit(solution)/shard_map/ppermute | solution.py:34
  144.8 5.9 %collective-permute-start.18 = (f32[3,1,2,2,128]{4,3,2,1,0:T(2,128)S(1)}, f32[3,1,2,2,128]{4,3,2,1,0:T(2,128)S(1)}, u32[]{:S(2)}, u32[]{:S(2)}) collective-permute-start(f32[3,1,2,2,128]{4,3,2,1,0:T(2,128)S(1)} %get-tuple-element.1027), channel_id=1, source_target_pairs={{0,16},{16,32},{32,48},{48,64},{64,80},{80,96},{96,112},{112,128},... | collective-permute-start | bytes 18440 | tf_op jit(solution)/shard_map/ppermute | solution.py:31
  148.8 6.4 %collective-permute-start.19 = (f32[3,1,2,2,128]{4,3,2,1,0:T(2,128)S(1)}, f32[3,1,2,2,128]{4,3,2,1,0:T(2,128)S(1)}, u32[]{:S(2)}, u32[]{:S(2)}) collective-permute-start(f32[3,1,2,2,128]{4,3,2,1,0:T(2,128)S(1)} %get-tuple-element.1028), channel_id=1, source_target_pairs={{16,0},{32,16},{48,32},{64,48},{80,64},{96,80},{112,96},{128,112},... | collective-permute-start | bytes 18440 | tf_op jit(solution)/shard_map/ppermute | solution.py:34
  155.2 9.4 %collective-permute-start.21 = (f32[3,4,1,2,128]{4,3,2,1,0:T(2,128)S(1)}, f32[3,4,1,2,128]{4,3,2,1,0:T(2,128)S(1)}, u32[]{:S(2)}, u32[]{:S(2)}) collective-permute-start(f32[3,4,1,2,128]{4,3,2,1,0:T(2,128)S(1)} %get-tuple-element.975), channel_id=1, source_target_pairs={{4,0},{8,4},{12,8},{5,1},{9,5},{13,9},{6,2},{10,6},{14,10},{7,3},{... | collective-permute-start | bytes 36872 | tf_op jit(solution)/shard_map/ppermute | solution.py:34
  156.5 8.2 %collective-permute-start.20 = (f32[3,4,1,2,128]{4,3,2,1,0:T(2,128)S(1)}, f32[3,4,1,2,128]{4,3,2,1,0:T(2,128)S(1)}, u32[]{:S(2)}, u32[]{:S(2)}) collective-permute-start(f32[3,4,1,2,128]{4,3,2,1,0:T(2,128)S(1)} %get-tuple-element.976), channel_id=1, source_target_pairs={{0,4},{4,8},{8,12},{1,5},{5,9},{9,13},{2,6},{6,10},{10,14},{3,7},{... | collective-permute-start | bytes 36872 | tf_op jit(solution)/shard_map/ppermute | solution.py:31
  164.8 17.0 %collective-permute-start.23 = (f32[3,4,4,1,128]{4,3,2,1,0:T(1,128)S(1)}, f32[3,4,4,1,128]{4,3,2,1,0:T(1,128)S(1)}, u32[]{:S(2)}, u32[]{:S(2)}) collective-permute-start(f32[3,4,4,1,128]{4,3,2,1,0:T(1,128)S(1)} %get-tuple-element.861), channel_id=1, source_target_pairs={{1,0},{2,1},{3,2},{5,4},{6,5},{7,6},{9,8},{10,9},{11,10},{13,12},{... | collective-permute-start | bytes 73736 | tf_op jit(solution)/shard_map/ppermute | solution.py:34
  166.7 15.1 %collective-permute-start.22 = (f32[3,4,4,1,128]{4,3,2,1,0:T(1,128)S(1)}, f32[3,4,4,1,128]{4,3,2,1,0:T(1,128)S(1)}, u32[]{:S(2)}, u32[]{:S(2)}) collective-permute-start(f32[3,4,4,1,128]{4,3,2,1,0:T(1,128)S(1)} %get-tuple-element.862), channel_id=1, source_target_pairs={{0,1},{1,2},{2,3},{4,5},{5,6},{6,7},{8,9},{9,10},{10,11},{12,13},{... | collective-permute-start | bytes 73736 | tf_op jit(solution)/shard_map/ppermute | solution.py:31
  215.3 5.9 %collective-permute-start.24 = (f32[1,1,2,2,128]{4,3,2,1,0:T(2,128)S(1)}, f32[1,1,2,2,128]{4,3,2,1,0:T(2,128)S(1)}, u32[]{:S(2)}, u32[]{:S(2)}) collective-permute-start(f32[1,1,2,2,128]{4,3,2,1,0:T(2,128)S(1)} %get-tuple-element.1053), channel_id=1, source_target_pairs={{0,16},{16,32},{32,48},{48,64},{64,80},{80,96},{96,112},{112,128},... | collective-permute-start | bytes 6152 | tf_op jit(solution)/shard_map/ppermute | solution.py:31
  218.5 7.5 %collective-permute-start.25 = (f32[1,1,2,2,128]{4,3,2,1,0:T(2,128)S(1)}, f32[1,1,2,2,128]{4,3,2,1,0:T(2,128)S(1)}, u32[]{:S(2)}, u32[]{:S(2)}) collective-permute-start(f32[1,1,2,2,128]{4,3,2,1,0:T(2,128)S(1)} %get-tuple-element.1054), channel_id=1, source_target_pairs={{16,0},{32,16},{48,32},{64,48},{80,64},{96,80},{112,96},{128,112},... | collective-permute-start | bytes 6152 | tf_op jit(solution)/shard_map/ppermute | solution.py:34
  226.1 5.2 %collective-permute-start.26 = (f32[1,4,1,2,128]{4,3,2,1,0:T(2,128)S(1)}, f32[1,4,1,2,128]{4,3,2,1,0:T(2,128)S(1)}, u32[]{:S(2)}, u32[]{:S(2)}) collective-permute-start(f32[1,4,1,2,128]{4,3,2,1,0:T(2,128)S(1)} %get-tuple-element.1041), channel_id=1, source_target_pairs={{0,4},{4,8},{8,12},{1,5},{5,9},{9,13},{2,6},{6,10},{10,14},{3,7},{... | collective-permute-start | bytes 12296 | tf_op jit(solution)/shard_map/ppermute | solution.py:31
  230.0 5.5 %collective-permute-start.27 = (f32[1,4,1,2,128]{4,3,2,1,0:T(2,128)S(1)}, f32[1,4,1,2,128]{4,3,2,1,0:T(2,128)S(1)}, u32[]{:S(2)}, u32[]{:S(2)}) collective-permute-start(f32[1,4,1,2,128]{4,3,2,1,0:T(2,128)S(1)} %get-tuple-element.1042), channel_id=1, source_target_pairs={{4,0},{8,4},{12,8},{5,1},{9,5},{13,9},{6,2},{10,6},{14,10},{7,3},{... | collective-permute-start | bytes 12296 | tf_op jit(solution)/shard_map/ppermute | solution.py:34
  235.5 4.4 %collective-permute-start.29 = (f32[1,4,4,1,128]{4,3,2,1,0:T(1,128)S(1)}, f32[1,4,4,1,128]{4,3,2,1,0:T(1,128)S(1)}, u32[]{:S(2)}, u32[]{:S(2)}) collective-permute-start(f32[1,4,4,1,128]{4,3,2,1,0:T(1,128)S(1)} %get-tuple-element.995), channel_id=1, source_target_pairs={{1,0},{2,1},{3,2},{5,4},{6,5},{7,6},{9,8},{10,9},{11,10},{13,12},{... | collective-permute-start | bytes 24584 | tf_op jit(solution)/shard_map/ppermute | solution.py:34
  237.6 6.5 %collective-permute-start.28 = (f32[1,4,4,1,128]{4,3,2,1,0:T(1,128)S(1)}, f32[1,4,4,1,128]{4,3,2,1,0:T(1,128)S(1)}, u32[]{:S(2)}, u32[]{:S(2)}) collective-permute-start(f32[1,4,4,1,128]{4,3,2,1,0:T(1,128)S(1)} %get-tuple-element.996), channel_id=1, source_target_pairs={{0,1},{1,2},{2,3},{4,5},{5,6},{6,7},{8,9},{9,10},{10,11},{12,13},{... | collective-permute-start | bytes 24584 | tf_op jit(solution)/shard_map/ppermute | solution.py:31
  270.7 5.9 %collective-permute-start.30 = (f32[3,1,2,2,128]{4,3,2,1,0:T(2,128)S(1)}, f32[3,1,2,2,128]{4,3,2,1,0:T(2,128)S(1)}, u32[]{:S(2)}, u32[]{:S(2)}) collective-permute-start(f32[3,1,2,2,128]{4,3,2,1,0:T(2,128)S(1)} %get-tuple-element.1013), channel_id=1, source_target_pairs={{0,16},{16,32},{32,48},{48,64},{64,80},{80,96},{96,112},{112,128},... | collective-permute-start | bytes 18440 | tf_op jit(solution)/shard_map/ppermute | solution.py:31
  274.6 6.7 %collective-permute-start.31 = (f32[3,1,2,2,128]{4,3,2,1,0:T(2,128)S(1)}, f32[3,1,2,2,128]{4,3,2,1,0:T(2,128)S(1)}, u32[]{:S(2)}, u32[]{:S(2)}) collective-permute-start(f32[3,1,2,2,128]{4,3,2,1,0:T(2,128)S(1)} %get-tuple-element.1014), channel_id=1, source_target_pairs={{16,0},{32,16},{48,32},{64,48},{80,64},{96,80},{112,96},{128,112},... | collective-permute-start | bytes 18440 | tf_op jit(solution)/shard_map/ppermute | solution.py:34
  281.4 5.9 %collective-permute-start.32 = (f32[3,4,1,2,128]{4,3,2,1,0:T(2,128)S(1)}, f32[3,4,1,2,128]{4,3,2,1,0:T(2,128)S(1)}, u32[]{:S(2)}, u32[]{:S(2)}) collective-permute-start(f32[3,4,1,2,128]{4,3,2,1,0:T(2,128)S(1)} %get-tuple-element.971), channel_id=1, source_target_pairs={{0,4},{4,8},{8,12},{1,5},{5,9},{9,13},{2,6},{6,10},{10,14},{3,7},{... | collective-permute-start | bytes 36872 | tf_op jit(solution)/shard_map/ppermute | solution.py:31
  283.6 5.6 %collective-permute-start.33 = (f32[3,4,1,2,128]{4,3,2,1,0:T(2,128)S(1)}, f32[3,4,1,2,128]{4,3,2,1,0:T(2,128)S(1)}, u32[]{:S(2)}, u32[]{:S(2)}) collective-permute-start(f32[3,4,1,2,128]{4,3,2,1,0:T(2,128)S(1)} %get-tuple-element.972), channel_id=1, source_target_pairs={{4,0},{8,4},{12,8},{5,1},{9,5},{13,9},{6,2},{10,6},{14,10},{7,3},{... | collective-permute-start | bytes 36872 | tf_op jit(solution)/shard_map/ppermute | solution.py:34
  289.3 15.1 %collective-permute-start.34 = (f32[3,4,4,1,128]{4,3,2,1,0:T(1,128)S(1)}, f32[3,4,4,1,128]{4,3,2,1,0:T(1,128)S(1)}, u32[]{:S(2)}, u32[]{:S(2)}) collective-permute-start(f32[3,4,4,1,128]{4,3,2,1,0:T(1,128)S(1)} %get-tuple-element.857), channel_id=1, source_target_pairs={{0,1},{1,2},{2,3},{4,5},{5,6},{6,7},{8,9},{9,10},{10,11},{12,13},{... | collective-permute-start | bytes 73736 | tf_op jit(solution)/shard_map/ppermute | solution.py:31
  291.2 13.1 %collective-permute-start.35 = (f32[3,4,4,1,128]{4,3,2,1,0:T(1,128)S(1)}, f32[3,4,4,1,128]{4,3,2,1,0:T(1,128)S(1)}, u32[]{:S(2)}, u32[]{:S(2)}) collective-permute-start(f32[3,4,4,1,128]{4,3,2,1,0:T(1,128)S(1)} %get-tuple-element.858), channel_id=1, source_target_pairs={{1,0},{2,1},{3,2},{5,4},{6,5},{7,6},{9,8},{10,9},{11,10},{13,12},{... | collective-permute-start | bytes 73736 | tf_op jit(solution)/shard_map/ppermute | solution.py:34
  351.9 24.2 %collective-permute-start.36 = (f32[1,1,2,2,128]{4,3,2,1,0:T(2,128)S(1)}, f32[1,1,2,2,128]{4,3,2,1,0:T(2,128)S(1)}, u32[]{:S(2)}, u32[]{:S(2)}) collective-permute-start(f32[1,1,2,2,128]{4,3,2,1,0:T(2,128)S(1)} %get-tuple-element.1049), channel_id=1, source_target_pairs={{0,16},{16,32},{32,48},{48,64},{64,80},{80,96},{96,112},{112,128},... | collective-permute-start | bytes 6152 | tf_op jit(solution)/shard_map/ppermute | solution.py:31
  353.8 22.3 %collective-permute-start.37 = (f32[1,1,2,2,128]{4,3,2,1,0:T(2,128)S(1)}, f32[1,1,2,2,128]{4,3,2,1,0:T(2,128)S(1)}, u32[]{:S(2)}, u32[]{:S(2)}) collective-permute-start(f32[1,1,2,2,128]{4,3,2,1,0:T(2,128)S(1)} %get-tuple-element.1050), channel_id=1, source_target_pairs={{16,0},{32,16},{48,32},{64,48},{80,64},{96,80},{112,96},{128,112},... | collective-permute-start | bytes 6152 | tf_op jit(solution)/shard_map/ppermute | solution.py:34
  376.1 4.4 %collective-permute-start.38 = (f32[1,4,1,2,128]{4,3,2,1,0:T(2,128)S(1)}, f32[1,4,1,2,128]{4,3,2,1,0:T(2,128)S(1)}, u32[]{:S(2)}, u32[]{:S(2)}) collective-permute-start(f32[1,4,1,2,128]{4,3,2,1,0:T(2,128)S(1)} %get-tuple-element.1037), channel_id=1, source_target_pairs={{0,4},{4,8},{8,12},{1,5},{5,9},{9,13},{2,6},{6,10},{10,14},{3,7},{... | collective-permute-start | bytes 12296 | tf_op jit(solution)/shard_map/ppermute | solution.py:31
  379.3 5.5 %collective-permute-start.39 = (f32[1,4,1,2,128]{4,3,2,1,0:T(2,128)S(1)}, f32[1,4,1,2,128]{4,3,2,1,0:T(2,128)S(1)}, u32[]{:S(2)}, u32[]{:S(2)}) collective-permute-start(f32[1,4,1,2,128]{4,3,2,1,0:T(2,128)S(1)} %get-tuple-element.1038), channel_id=1, source_target_pairs={{4,0},{8,4},{12,8},{5,1},{9,5},{13,9},{6,2},{10,6},{14,10},{7,3},{... | collective-permute-start | bytes 12296 | tf_op jit(solution)/shard_map/ppermute | solution.py:34
  384.8 4.4 %collective-permute-start.41 = (f32[1,4,4,1,128]{4,3,2,1,0:T(1,128)S(1)}, f32[1,4,4,1,128]{4,3,2,1,0:T(1,128)S(1)}, u32[]{:S(2)}, u32[]{:S(2)}) collective-permute-start(f32[1,4,4,1,128]{4,3,2,1,0:T(1,128)S(1)} %get-tuple-element.991), channel_id=1, source_target_pairs={{1,0},{2,1},{3,2},{5,4},{6,5},{7,6},{9,8},{10,9},{11,10},{13,12},{... | collective-permute-start | bytes 24584 | tf_op jit(solution)/shard_map/ppermute | solution.py:34
  386.7 6.5 %collective-permute-start.40 = (f32[1,4,4,1,128]{4,3,2,1,0:T(1,128)S(1)}, f32[1,4,4,1,128]{4,3,2,1,0:T(1,128)S(1)}, u32[]{:S(2)}, u32[]{:S(2)}) collective-permute-start(f32[1,4,4,1,128]{4,3,2,1,0:T(1,128)S(1)} %get-tuple-element.992), channel_id=1, source_target_pairs={{0,1},{1,2},{2,3},{4,5},{5,6},{6,7},{8,9},{9,10},{10,11},{12,13},{... | collective-permute-start | bytes 24584 | tf_op jit(solution)/shard_map/ppermute | solution.py:31
  (3 other events, 2.0 us)
where the time goes:
time: 427 us; the launch traced here: 421 us
  other arithmetic  204 us (48%)
  starting transfers between devices  111 us (26%)
  waiting for transfers between devices  53.5 us (13%)
  blocking collectives  40.7 us (10%)
  local copies, waits for them, and re-layouts  6.64 us (2%)
  between operations  4.63 us (1%)
    reduce_sum x44, other arithmetic, accel_pass(): totals = [totals[k] + jnp.sum(factor * grads[k], -1) for k in range(3)]  98.7 us
    reduce_sum x51, other arithmetic, apply_pass(): total = total + jnp.sum(masses * closing, -1)  78.3 us
    ppermute x18, starting transfers between devices, with_halo(): lax.ppermute(lax.slice_in_dim(block, block.shape[dim] - width, None, axis...  53.6 us
    ppermute x18, starting transfers between devices, with_halo(): lax.ppermute(lax.slice_in_dim(block, 0, width, axis=dim), axis, backward)  41.5 us
    psum x5, blocking collectives, one_axis_at_a_time(): x = lax.psum(x, axis)  40.7 us
    ppermute x18, waiting for transfers between devices, with_halo(): lax.ppermute(lax.slice_in_dim(block, 0, width, axis=dim), axis, backward)  35.4 us
    ppermute x6, starting transfers between devices, passed_along(): return lax.ppermute(x, axis, pairs)  16.1 us
    ppermute x18, waiting for transfers between devices, with_halo(): lax.ppermute(lax.slice_in_dim(block, block.shape[dim] - width, None, axis...  12.4 us
  transfers between devices with their start and end apart: 42, of which 16 were waited for; matrix products, arithmetic and copies ran while one was open for 10% of the time, Pallas kernels for 0%

commit v1 on v0

--- a/solution.py
+++ b/solution.py
@@ -38,7 +38,7 @@
 
 def one_axis_at_a_time(x, axes):
     for axis in axes:
-        x = lax.psum(x, axis)
+        x = jnp.sum(lax.all_gather(x, axis), axis=0)
     return x
 
 

time: 427 us -> 432 us (1.012)
  local copies, waits for them, and re-layouts: 6.64 us -> 11.8 us
  waiting for transfers between devices: 53.5 us -> 48.7 us
    unnamed x0 -> x5, blocking collectives: none -> 41.3 us
    psum x5 -> x0, blocking collectives: 40.7 us -> none  [one_axis_at_a_time(): x = lax.psum(x, axis)]
    ppermute x18, waiting for transfers between devices: 35.4 us -> 30.6 us  [with_halo(): lax.ppermute(lax.slice_in_dim(block, 0, width, axis=dim), axis, backward)]
    unnamed x23 -> x47, local copies, waits for them, and re-layouts: 2.68 us -> 7.45 us
  transfers between devices with their start and end apart: 42 -> 42, of which waited for: 16 -> 15; matrix products, arithmetic and copies ran while one was open for 10% -> 11% of each run, Pallas kernels for 0% -> 0%
where the time goes in v1:
time: 432 us; the launch traced here: 426 us
  other arithmetic  205 us (47%)
  starting transfers between devices  111 us (26%)
  waiting for transfers between devices  48.7 us (11%)
  blocking collectives  41.3 us (10%)
  local copies, waits for them, and re-layouts  11.8 us (3%)
  between operations  7.97 us (2%)
    reduce_sum x44, other arithmetic, accel_pass(): totals = [totals[k] + jnp.sum(factor * grads[k], -1) for k in range(3)]  98.7 us
    reduce_sum x51, other arithmetic, apply_pass(): total = total + jnp.sum(masses * closing, -1)  78.3 us
    ppermute x18, starting transfers between devices, with_halo(): lax.ppermute(lax.slice_in_dim(block, block.shape[dim] - width, None, axis...  54.5 us
    unnamed x5, blocking collectives  41.3 us
    ppermute x18, starting transfers between devices, with_halo(): lax.ppermute(lax.slice_in_dim(block, 0, width, axis=dim), axis, backward)  40.7 us
    ppermute x18, waiting for transfers between devices, with_halo(): lax.ppermute(lax.slice_in_dim(block, 0, width, axis=dim), axis, backward)  30.6 us
    ppermute x6, starting transfers between devices, passed_along(): return lax.ppermute(x, axis, pairs)  16.1 us
    ppermute x18, waiting for transfers between devices, with_halo(): lax.ppermute(lax.slice_in_dim(block, block.shape[dim] - width, None, axis...  12.4 us
  transfers between devices with their start and end apart: 42, of which 15 were waited for; matrix products, arithmetic and copies ran while one was open for 11% of the time, Pallas kernels for 0%

profile of v1, /device:TPU:24, one launch (start us, length us, event | category | flops | bytes accessed | tf_op | source)
XLA Modules:
  0.0 426.1 jit_solution(6240603301443907932)
XLA Ops:
  8.5 4.5 %collective-permute-start.2 = (f32[7,1,1,1,128]{4,3,2,1,0:T(1,128)S(1)}, f32[7,1,1,1,128]{4,3,2,1,0:T(1,128)S(1)}, u32[]{:S(2)}, u32[]{:S(2)}) collective-permute-start(f32[7,1,1,1,128]{4,3,2,1,0:T(1,128)S(1)} %get-tuple-element.1061), channel_id=1, source_target_pairs={{0,4},{4,8},{8,12},{1,5},{5,9},{9,13},{2,6},{6,10},{10,14},{3,7},{... | collective-permute-start | bytes 10760 | tf_op jit(solution)/shard_map/ppermute | solution.py:23
  13.1 3.8 collective-permute-start
  20.5 4.5 %collective-permute-done.1 = f32[7,1,1,1,128]{4,3,2,1,0:T(1,128)S(1)} collective-permute-done((f32[7,1,1,1,128]{4,3,2,1,0:T(1,128)S(1)}, f32[7,1,1,1,128]{4,3,2,1,0:T(1,128)S(1)}, u32[]{:S(2)}, u32[]{:S(2)}) %collective-permute-start.1) | collective-permute-done | bytes 3616 | tf_op jit(solution)/shard_map/ppermute | solution.py:23
  27.9 6.9 %scatter_custom_fusion = f32[1025,6]{1,0:T(8,128)S(1)} fusion(s32[768]{0:T(1024)S(1)} %fusion.171, f32[6,1,1,1,768]{0,4,1,2,3:T(8,128)S(1)} %copy.31, f32[]{:T(128)} %constant.125.clone.1), kind=kCustom, calls=%fused_computation.810 | custom fusion | flops 4608 | bytes 417820 | tf_op jit(solution)/shard_map/scatter-add | solution.py:149
  35.2 3.8 collective-permute-start.6
  42.7 2.9 collective-permute-done.7
  45.6 3.2 collective-permute-start.8
  50.4 4.2 collective-permute-done.9
  59.7 4.0 collective-permute-done.10
  79.1 3.1 collective-permute-start.13
  82.2 3.2 collective-permute-done.13
  85.5 3.3 collective-permute-start.14
  96.3 5.3 %collective-permute-start.17 = (f32[1,4,4,1,128]{4,3,2,1,0:T(1,128)S(1)}, f32[1,4,4,1,128]{4,3,2,1,0:T(1,128)S(1)}, u32[]{:S(2)}, u32[]{:S(2)}) collective-permute-start(f32[1,4,4,1,128]{4,3,2,1,0:T(1,128)S(1)} %get-tuple-element.1000), channel_id=1, source_target_pairs={{1,0},{2,1},{3,2},{5,4},{6,5},{7,6},{9,8},{10,9},{11,10},{13,12},{... | collective-permute-start | bytes 24584 | tf_op jit(solution)/shard_map/ppermute | solution.py:34
  144.8 3.9 collective-permute-start.18
  150.7 4.5 %collective-permute-done.19 = f32[3,1,2,2,128]{4,3,2,1,0:T(2,128)S(1)} collective-permute-done((f32[3,1,2,2,128]{4,3,2,1,0:T(2,128)S(1)}, f32[3,1,2,2,128]{4,3,2,1,0:T(2,128)S(1)}, u32[]{:S(2)}, u32[]{:S(2)}) %collective-permute-start.19) | collective-permute-done | bytes 6176 | tf_op jit(solution)/shard_map/ppermute | solution.py:34
  156.5 4.5 %collective-permute-start.20 = (f32[3,4,1,2,128]{4,3,2,1,0:T(2,128)S(1)}, f32[3,4,1,2,128]{4,3,2,1,0:T(2,128)S(1)}, u32[]{:S(2)}, u32[]{:S(2)}) collective-permute-start(f32[3,4,1,2,128]{4,3,2,1,0:T(2,128)S(1)} %get-tuple-element.976), channel_id=1, source_target_pairs={{0,4},{4,8},{8,12},{1,5},{5,9},{9,13},{2,6},{6,10},{10,14},{3,7},{... | collective-permute-start | bytes 36872 | tf_op jit(solution)/shard_map/ppermute | solution.py:31
  176.7 3.3 multiply_reduce_fusion.349
  215.3 3.2 collective-permute-start.24
  221.2 4.9 %collective-permute-done.25 = f32[1,1,2,2,128]{4,3,2,1,0:T(2,128)S(1)} collective-permute-done((f32[1,1,2,2,128]{4,3,2,1,0:T(2,128)S(1)}, f32[1,1,2,2,128]{4,3,2,1,0:T(2,128)S(1)}, u32[]{:S(2)}, u32[]{:S(2)}) %collective-permute-start.25) | collective-permute-done | bytes 2080 | tf_op jit(solution)/shard_map/ppermute | solution.py:34
  226.1 3.9 collective-permute-start.26
  231.4 4.2 collective-permute-done.27
  240.0 4.2 collective-permute-done.28
  244.2 3.1 multiply_reduce_fusion.175
  247.3 2.9 multiply_reduce_fusion.187
  250.2 2.9 multiply_reduce_fusion.164
  253.1 2.9 multiply_reduce_fusion.167
  256.1 2.9 multiply_reduce_fusion.170
  258.9 2.9 multiply_reduce_fusion.179
  261.8 2.9 multiply_reduce_fusion.182
  267.6 2.9 multiply_reduce_fusion.176
  270.7 3.9 collective-permute-start.30
  292.9 5.1 %collective-permute-start.35 = (f32[3,4,4,1,128]{4,3,2,1,0:T(1,128)S(1)}, f32[3,4,4,1,128]{4,3,2,1,0:T(1,128)S(1)}, u32[]{:S(2)}, u32[]{:S(2)}) collective-permute-start(f32[3,4,4,1,128]{4,3,2,1,0:T(1,128)S(1)} %get-tuple-element.858), channel_id=1, source_target_pairs={{1,0},{2,1},{3,2},{5,4},{6,5},{7,6},{9,8},{10,9},{11,10},{13,12},{... | collective-permute-start | bytes 73736 | tf_op jit(solution)/shard_map/ppermute | solution.py:34
  330.2 19.0 %all-reduce = f32[16]{0:T(128)S(1)} all-reduce(f32[16]{0:T(128)S(1)} %maximum_dynamic-update-slice_fusion), channel_id=2, replica_groups=mesh['gx_0'=8,'gx_1'=2,'gy'=4,'gz_0'=2,'gz_1'=2] {'gx_0'}, use_global_device_ids=true, to_apply=%add | all-reduce | flops 16 | bytes 128
  350.2 4.9 %all-reduce.1 = f32[4]{0:T(128)S(1)} all-reduce(f32[4]{0:T(128)S(1)} %dynamic-update-slice.1), channel_id=3, replica_groups=mesh['gx_0'=8,'gx_1'=2,'gy'=4,'gz_0'=2,'gz_1'=2] {'gx_1'}, use_global_device_ids=true, to_apply=%add.1 | all-reduce | flops 4 | bytes 32
  358.7 3.0 collective-permute-start.37
  362.1 8.5 %all-reduce.2 = f32[8]{0:T(128)S(1)} all-reduce(f32[8]{0:T(128)S(1)} %dynamic-update-slice.2), channel_id=4, replica_groups=mesh['gx_0'=8,'gx_1'=2,'gy'=4,'gz_0'=2,'gz_1'=2] {'gy'}, use_global_device_ids=true, to_apply=%add.2 | all-reduce | flops 8 | bytes 64
  371.2 6.4 %all-reduce.3 = f32[4]{0:T(128)S(1)} all-reduce(f32[4]{0:T(128)S(1)} %dynamic-update-slice.3), channel_id=5, replica_groups=mesh['gx_0'=8,'gx_1'=2,'gy'=4,'gz_0'=2,'gz_1'=2] {'gz_0'}, use_global_device_ids=true, to_apply=%add.3 | all-reduce | flops 4 | bytes 32
  381.2 3.1 collective-permute-start.38
  385.7 4.2 collective-permute-done.39
  394.3 4.0 collective-permute-done.40
  398.4 2.9 multiply_reduce_fusion.67
  404.2 2.9 multiply_reduce_fusion.74
  407.1 2.9 multiply_reduce_fusion.71
  410.0 2.9 multiply_reduce_fusion.68
  412.9 2.9 multiply_reduce_fusion.62
  415.8 2.9 multiply_reduce_fusion.59
  418.7 2.9 multiply_reduce_fusion.79
  421.6 2.9 multiply_reduce_fusion.56
  (332 shorter events, 219.9 us)
Async XLA Ops:
  2.0 0.7 copy-start.4
  2.7 22.4 %collective-permute-start.5 = (f32[7,1,1,1,128]{4,3,2,1,0:T(1,128)S(1)}, f32[7,1,1,1,128]{4,3,2,1,0:T(1,128)S(1)}, u32[]{:S(2)}, u32[]{:S(2)}) collective-permute-start(f32[7,1,1,1,128]{4,3,2,1,0:T(1,128)S(1)} %get-tuple-element.569), channel_id=1, source_target_pairs={{1,0},{2,1},{3,2},{5,4},{6,5},{7,6},{9,8},{10,9},{11,10},{13,12},{... | collective-permute-start | bytes 10760 | tf_op jit(solution)/shard_map/ppermute | solution.py:23
  5.2 11.8 %copy-start.2 = (f32[3,2,2,2,128]{4,3,2,1,0:T(2,128)S(1)}, f32[3,2,2,2,128]{4,3,2,1,0:T(2,128)}, u32[]{:S(2)}) copy-start(f32[3,2,2,2,128]{4,3,2,1,0:T(2,128)} %param.11) | copy-start | bytes 36868
  5.3 11.8 %copy-start.3 = (f32[3,2,2,2,128]{4,3,2,1,0:T(2,128)S(1)}, f32[3,2,2,2,128]{4,3,2,1,0:T(2,128)}, u32[]{:S(2)}) copy-start(f32[3,2,2,2,128]{4,3,2,1,0:T(2,128)} %param.10) | copy-start | bytes 36868
  5.3 19.7 %collective-permute-start.4 = (f32[7,1,1,1,128]{4,3,2,1,0:T(1,128)S(1)}, f32[7,1,1,1,128]{4,3,2,1,0:T(1,128)S(1)}, u32[]{:S(2)}, u32[]{:S(2)}) collective-permute-start(f32[7,1,1,1,128]{4,3,2,1,0:T(1,128)S(1)} %get-tuple-element.1059), channel_id=1, source_target_pairs={{0,1},{1,2},{2,3},{4,5},{5,6},{6,7},{8,9},{9,10},{10,11},{12,13},{... | collective-permute-start | bytes 10760 | tf_op jit(solution)/shard_map/ppermute | solution.py:23
  7.2 9.7 %copy-start = (s32[2,2,2]{2,1,0:T(2,128)S(1)}, s32[2,2,2]{2,1,0:T(2,128)}, u32[]{:S(2)}) copy-start(s32[2,2,2]{2,1,0:T(2,128)} %param.13) | copy-start | bytes 100
  7.2 17.8 %collective-permute-start.3 = (f32[7,1,1,1,128]{4,3,2,1,0:T(1,128)S(1)}, f32[7,1,1,1,128]{4,3,2,1,0:T(1,128)S(1)}, u32[]{:S(2)}, u32[]{:S(2)}) collective-permute-start(f32[7,1,1,1,128]{4,3,2,1,0:T(1,128)S(1)} %get-tuple-element.1060), channel_id=1, source_target_pairs={{4,0},{8,4},{12,8},{5,1},{9,5},{13,9},{6,2},{10,6},{14,10},{7,3},{... | collective-permute-start | bytes 10760 | tf_op jit(solution)/shard_map/ppermute | solution.py:23
  8.5 16.4 %collective-permute-start.2 = (f32[7,1,1,1,128]{4,3,2,1,0:T(1,128)S(1)}, f32[7,1,1,1,128]{4,3,2,1,0:T(1,128)S(1)}, u32[]{:S(2)}, u32[]{:S(2)}) collective-permute-start(f32[7,1,1,1,128]{4,3,2,1,0:T(1,128)S(1)} %get-tuple-element.1061), channel_id=1, source_target_pairs={{0,4},{4,8},{8,12},{1,5},{5,9},{9,13},{2,6},{6,10},{10,14},{3,7},{... | collective-permute-start | bytes 10760 | tf_op jit(solution)/shard_map/ppermute | solution.py:23
  13.1 5.5 %collective-permute-start = (f32[7,1,1,1,128]{4,3,2,1,0:T(1,128)S(1)}, f32[7,1,1,1,128]{4,3,2,1,0:T(1,128)S(1)}, u32[]{:S(2)}, u32[]{:S(2)}) collective-permute-start(f32[7,1,1,1,128]{4,3,2,1,0:T(1,128)S(1)} %get-tuple-element.1063), channel_id=1, source_target_pairs={{0,16},{16,32},{32,48},{48,64},{64,80},{80,96},{96,112},{112,128},... | collective-permute-start | bytes 10760 | tf_op jit(solution)/shard_map/ppermute | solution.py:23
  18.6 6.4 %collective-permute-start.1 = (f32[7,1,1,1,128]{4,3,2,1,0:T(1,128)S(1)}, f32[7,1,1,1,128]{4,3,2,1,0:T(1,128)S(1)}, u32[]{:S(2)}, u32[]{:S(2)}) collective-permute-start(f32[7,1,1,1,128]{4,3,2,1,0:T(1,128)S(1)} %get-tuple-element.1062), channel_id=1, source_target_pairs={{16,0},{32,16},{48,32},{64,48},{80,64},{96,80},{112,96},{128,112},... | collective-permute-start | bytes 10760 | tf_op jit(solution)/shard_map/ppermute | solution.py:23
  35.2 7.4 %collective-permute-start.6 = (f32[7,1,2,2,128]{4,3,2,1,0:T(2,128)S(1)}, f32[7,1,2,2,128]{4,3,2,1,0:T(2,128)S(1)}, u32[]{:S(2)}, u32[]{:S(2)}) collective-permute-start(f32[7,1,2,2,128]{4,3,2,1,0:T(2,128)S(1)} %get-tuple-element.967), channel_id=1, source_target_pairs={{0,16},{16,32},{32,48},{48,64},{64,80},{80,96},{96,112},{112,128},... | collective-permute-start | bytes 43016 | tf_op jit(solution)/shard_map/ppermute | solution.py:31
  39.1 6.5 %collective-permute-start.7 = (f32[7,1,2,2,128]{4,3,2,1,0:T(2,128)S(1)}, f32[7,1,2,2,128]{4,3,2,1,0:T(2,128)S(1)}, u32[]{:S(2)}, u32[]{:S(2)}) collective-permute-start(f32[7,1,2,2,128]{4,3,2,1,0:T(2,128)S(1)} %get-tuple-element.968), channel_id=1, source_target_pairs={{16,0},{32,16},{48,32},{64,48},{80,64},{96,80},{112,96},{128,112},... | collective-permute-start | bytes 43016 | tf_op jit(solution)/shard_map/ppermute | solution.py:34
  45.6 4.8 %collective-permute-start.8 = (f32[7,4,1,2,128]{4,3,2,1,0:T(2,128)S(1)}, f32[7,4,1,2,128]{4,3,2,1,0:T(2,128)S(1)}, u32[]{:S(2)}, u32[]{:S(2)}) collective-permute-start(f32[7,4,1,2,128]{4,3,2,1,0:T(2,128)S(1)} %get-tuple-element.853), channel_id=1, source_target_pairs={{0,4},{4,8},{8,12},{1,5},{5,9},{9,13},{2,6},{6,10},{10,14},{3,7},{... | collective-permute-start | bytes 86024 | tf_op jit(solution)/shard_map/ppermute | solution.py:31
  48.9 5.8 %collective-permute-start.9 = (f32[7,4,1,2,128]{4,3,2,1,0:T(2,128)S(1)}, f32[7,4,1,2,128]{4,3,2,1,0:T(2,128)S(1)}, u32[]{:S(2)}, u32[]{:S(2)}) collective-permute-start(f32[7,4,1,2,128]{4,3,2,1,0:T(2,128)S(1)} %get-tuple-element.854), channel_id=1, source_target_pairs={{4,0},{8,4},{12,8},{5,1},{9,5},{13,9},{6,2},{10,6},{14,10},{7,3},{... | collective-permute-start | bytes 86024 | tf_op jit(solution)/shard_map/ppermute | solution.py:34
  54.8 5.0 %collective-permute-start.11 = (f32[7,4,4,1,128]{4,3,2,1,0:T(1,128)S(1)}, f32[7,4,4,1,128]{4,3,2,1,0:T(1,128)S(1)}, u32[]{:S(2)}, u32[]{:S(2)}) collective-permute-start(f32[7,4,4,1,128]{4,3,2,1,0:T(1,128)S(1)} %get-tuple-element.699), channel_id=1, source_target_pairs={{1,0},{2,1},{3,2},{5,4},{6,5},{7,6},{9,8},{10,9},{11,10},{13,12},{... | collective-permute-start | bytes 172040 | tf_op jit(solution)/shard_map/ppermute | solution.py:34
  56.7 7.0 %collective-permute-start.10 = (f32[7,4,4,1,128]{4,3,2,1,0:T(1,128)S(1)}, f32[7,4,4,1,128]{4,3,2,1,0:T(1,128)S(1)}, u32[]{:S(2)}, u32[]{:S(2)}) collective-permute-start(f32[7,4,4,1,128]{4,3,2,1,0:T(1,128)S(1)} %get-tuple-element.700), channel_id=1, source_target_pairs={{0,1},{1,2},{2,3},{4,5},{5,6},{6,7},{8,9},{9,10},{10,11},{12,13},{... | collective-permute-start | bytes 172040 | tf_op jit(solution)/shard_map/ppermute | solution.py:31
  75.5 0.7 copy-start.1
  76.3 5.9 %collective-permute-start.12 = (f32[1,1,2,2,128]{4,3,2,1,0:T(2,128)S(1)}, f32[1,1,2,2,128]{4,3,2,1,0:T(2,128)S(1)}, u32[]{:S(2)}, u32[]{:S(2)}) collective-permute-start(f32[1,1,2,2,128]{4,3,2,1,0:T(2,128)S(1)} %get-tuple-element.1057), channel_id=1, source_target_pairs={{0,16},{16,32},{32,48},{48,64},{64,80},{80,96},{96,112},{112,128},... | collective-permute-start | bytes 6152 | tf_op jit(solution)/shard_map/ppermute | solution.py:31
  79.1 6.4 %collective-permute-start.13 = (f32[1,1,2,2,128]{4,3,2,1,0:T(2,128)S(1)}, f32[1,1,2,2,128]{4,3,2,1,0:T(2,128)S(1)}, u32[]{:S(2)}, u32[]{:S(2)}) collective-permute-start(f32[1,1,2,2,128]{4,3,2,1,0:T(2,128)S(1)} %get-tuple-element.1058), channel_id=1, source_target_pairs={{16,0},{32,16},{48,32},{64,48},{80,64},{96,80},{112,96},{128,112},... | collective-permute-start | bytes 6152 | tf_op jit(solution)/shard_map/ppermute | solution.py:34
  85.5 8.2 %collective-permute-start.14 = (f32[1,4,1,2,128]{4,3,2,1,0:T(2,128)S(1)}, f32[1,4,1,2,128]{4,3,2,1,0:T(2,128)S(1)}, u32[]{:S(2)}, u32[]{:S(2)}) collective-permute-start(f32[1,4,1,2,128]{4,3,2,1,0:T(2,128)S(1)} %get-tuple-element.1045), channel_id=1, source_target_pairs={{0,4},{4,8},{8,12},{1,5},{5,9},{9,13},{2,6},{6,10},{10,14},{3,7},{... | collective-permute-start | bytes 12296 | tf_op jit(solution)/shard_map/ppermute | solution.py:31
  88.8 5.5 %collective-permute-start.15 = (f32[1,4,1,2,128]{4,3,2,1,0:T(2,128)S(1)}, f32[1,4,1,2,128]{4,3,2,1,0:T(2,128)S(1)}, u32[]{:S(2)}, u32[]{:S(2)}) collective-permute-start(f32[1,4,1,2,128]{4,3,2,1,0:T(2,128)S(1)} %get-tuple-element.1046), channel_id=1, source_target_pairs={{4,0},{8,4},{12,8},{5,1},{9,5},{13,9},{6,2},{10,6},{14,10},{7,3},{... | collective-permute-start | bytes 12296 | tf_op jit(solution)/shard_map/ppermute | solution.py:34
  94.3 17.9 %collective-permute-start.16 = (f32[1,4,4,1,128]{4,3,2,1,0:T(1,128)S(1)}, f32[1,4,4,1,128]{4,3,2,1,0:T(1,128)S(1)}, u32[]{:S(2)}, u32[]{:S(2)}) collective-permute-start(f32[1,4,4,1,128]{4,3,2,1,0:T(1,128)S(1)} %get-tuple-element.999), channel_id=1, source_target_pairs={{0,1},{1,2},{2,3},{4,5},{5,6},{6,7},{8,9},{9,10},{10,11},{12,13},{... | collective-permute-start | bytes 24584 | tf_op jit(solution)/shard_map/ppermute | solution.py:31
  96.3 16.0 %collective-permute-start.17 = (f32[1,4,4,1,128]{4,3,2,1,0:T(1,128)S(1)}, f32[1,4,4,1,128]{4,3,2,1,0:T(1,128)S(1)}, u32[]{:S(2)}, u32[]{:S(2)}) collective-permute-start(f32[1,4,4,1,128]{4,3,2,1,0:T(1,128)S(1)} %get-tuple-element.1000), channel_id=1, source_target_pairs={{1,0},{2,1},{3,2},{5,4},{6,5},{7,6},{9,8},{10,9},{11,10},{13,12},{... | collective-permute-start | bytes 24584 | tf_op jit(solution)/shard_map/ppermute | solution.py:34
  144.8 5.9 %collective-permute-start.18 = (f32[3,1,2,2,128]{4,3,2,1,0:T(2,128)S(1)}, f32[3,1,2,2,128]{4,3,2,1,0:T(2,128)S(1)}, u32[]{:S(2)}, u32[]{:S(2)}) collective-permute-start(f32[3,1,2,2,128]{4,3,2,1,0:T(2,128)S(1)} %get-tuple-element.1027), channel_id=1, source_target_pairs={{0,16},{16,32},{32,48},{48,64},{64,80},{80,96},{96,112},{112,128},... | collective-permute-start | bytes 18440 | tf_op jit(solution)/shard_map/ppermute | solution.py:31
  148.8 6.4 %collective-permute-start.19 = (f32[3,1,2,2,128]{4,3,2,1,0:T(2,128)S(1)}, f32[3,1,2,2,128]{4,3,2,1,0:T(2,128)S(1)}, u32[]{:S(2)}, u32[]{:S(2)}) collective-permute-start(f32[3,1,2,2,128]{4,3,2,1,0:T(2,128)S(1)} %get-tuple-element.1028), channel_id=1, source_target_pairs={{16,0},{32,16},{48,32},{64,48},{80,64},{96,80},{112,96},{128,112},... | collective-permute-start | bytes 18440 | tf_op jit(solution)/shard_map/ppermute | solution.py:34
  155.2 9.4 %collective-permute-start.21 = (f32[3,4,1,2,128]{4,3,2,1,0:T(2,128)S(1)}, f32[3,4,1,2,128]{4,3,2,1,0:T(2,128)S(1)}, u32[]{:S(2)}, u32[]{:S(2)}) collective-permute-start(f32[3,4,1,2,128]{4,3,2,1,0:T(2,128)S(1)} %get-tuple-element.975), channel_id=1, source_target_pairs={{4,0},{8,4},{12,8},{5,1},{9,5},{13,9},{6,2},{10,6},{14,10},{7,3},{... | collective-permute-start | bytes 36872 | tf_op jit(solution)/shard_map/ppermute | solution.py:34
  156.5 8.2 %collective-permute-start.20 = (f32[3,4,1,2,128]{4,3,2,1,0:T(2,128)S(1)}, f32[3,4,1,2,128]{4,3,2,1,0:T(2,128)S(1)}, u32[]{:S(2)}, u32[]{:S(2)}) collective-permute-start(f32[3,4,1,2,128]{4,3,2,1,0:T(2,128)S(1)} %get-tuple-element.976), channel_id=1, source_target_pairs={{0,4},{4,8},{8,12},{1,5},{5,9},{9,13},{2,6},{6,10},{10,14},{3,7},{... | collective-permute-start | bytes 36872 | tf_op jit(solution)/shard_map/ppermute | solution.py:31
  164.8 17.0 %collective-permute-start.23 = (f32[3,4,4,1,128]{4,3,2,1,0:T(1,128)S(1)}, f32[3,4,4,1,128]{4,3,2,1,0:T(1,128)S(1)}, u32[]{:S(2)}, u32[]{:S(2)}) collective-permute-start(f32[3,4,4,1,128]{4,3,2,1,0:T(1,128)S(1)} %get-tuple-element.861), channel_id=1, source_target_pairs={{1,0},{2,1},{3,2},{5,4},{6,5},{7,6},{9,8},{10,9},{11,10},{13,12},{... | collective-permute-start | bytes 73736 | tf_op jit(solution)/shard_map/ppermute | solution.py:34
  166.7 15.1 %collective-permute-start.22 = (f32[3,4,4,1,128]{4,3,2,1,0:T(1,128)S(1)}, f32[3,4,4,1,128]{4,3,2,1,0:T(1,128)S(1)}, u32[]{:S(2)}, u32[]{:S(2)}) collective-permute-start(f32[3,4,4,1,128]{4,3,2,1,0:T(1,128)S(1)} %get-tuple-element.862), channel_id=1, source_target_pairs={{0,1},{1,2},{2,3},{4,5},{5,6},{6,7},{8,9},{9,10},{10,11},{12,13},{... | collective-permute-start | bytes 73736 | tf_op jit(solution)/shard_map/ppermute | solution.py:31
  215.3 5.9 %collective-permute-start.24 = (f32[1,1,2,2,128]{4,3,2,1,0:T(2,128)S(1)}, f32[1,1,2,2,128]{4,3,2,1,0:T(2,128)S(1)}, u32[]{:S(2)}, u32[]{:S(2)}) collective-permute-start(f32[1,1,2,2,128]{4,3,2,1,0:T(2,128)S(1)} %get-tuple-element.1053), channel_id=1, source_target_pairs={{0,16},{16,32},{32,48},{48,64},{64,80},{80,96},{96,112},{112,128},... | collective-permute-start | bytes 6152 | tf_op jit(solution)/shard_map/ppermute | solution.py:31
  218.5 7.5 %collective-permute-start.25 = (f32[1,1,2,2,128]{4,3,2,1,0:T(2,128)S(1)}, f32[1,1,2,2,128]{4,3,2,1,0:T(2,128)S(1)}, u32[]{:S(2)}, u32[]{:S(2)}) collective-permute-start(f32[1,1,2,2,128]{4,3,2,1,0:T(2,128)S(1)} %get-tuple-element.1054), channel_id=1, source_target_pairs={{16,0},{32,16},{48,32},{64,48},{80,64},{96,80},{112,96},{128,112},... | collective-permute-start | bytes 6152 | tf_op jit(solution)/shard_map/ppermute | solution.py:34
  226.1 5.2 %collective-permute-start.26 = (f32[1,4,1,2,128]{4,3,2,1,0:T(2,128)S(1)}, f32[1,4,1,2,128]{4,3,2,1,0:T(2,128)S(1)}, u32[]{:S(2)}, u32[]{:S(2)}) collective-permute-start(f32[1,4,1,2,128]{4,3,2,1,0:T(2,128)S(1)} %get-tuple-element.1041), channel_id=1, source_target_pairs={{0,4},{4,8},{8,12},{1,5},{5,9},{9,13},{2,6},{6,10},{10,14},{3,7},{... | collective-permute-start | bytes 12296 | tf_op jit(solution)/shard_map/ppermute | solution.py:31
  230.0 5.5 %collective-permute-start.27 = (f32[1,4,1,2,128]{4,3,2,1,0:T(2,128)S(1)}, f32[1,4,1,2,128]{4,3,2,1,0:T(2,128)S(1)}, u32[]{:S(2)}, u32[]{:S(2)}) collective-permute-start(f32[1,4,1,2,128]{4,3,2,1,0:T(2,128)S(1)} %get-tuple-element.1042), channel_id=1, source_target_pairs={{4,0},{8,4},{12,8},{5,1},{9,5},{13,9},{6,2},{10,6},{14,10},{7,3},{... | collective-permute-start | bytes 12296 | tf_op jit(solution)/shard_map/ppermute | solution.py:34
  235.6 4.4 %collective-permute-start.29 = (f32[1,4,4,1,128]{4,3,2,1,0:T(1,128)S(1)}, f32[1,4,4,1,128]{4,3,2,1,0:T(1,128)S(1)}, u32[]{:S(2)}, u32[]{:S(2)}) collective-permute-start(f32[1,4,4,1,128]{4,3,2,1,0:T(1,128)S(1)} %get-tuple-element.995), channel_id=1, source_target_pairs={{1,0},{2,1},{3,2},{5,4},{6,5},{7,6},{9,8},{10,9},{11,10},{13,12},{... | collective-permute-start | bytes 24584 | tf_op jit(solution)/shard_map/ppermute | solution.py:34
  237.7 6.5 %collective-permute-start.28 = (f32[1,4,4,1,128]{4,3,2,1,0:T(1,128)S(1)}, f32[1,4,4,1,128]{4,3,2,1,0:T(1,128)S(1)}, u32[]{:S(2)}, u32[]{:S(2)}) collective-permute-start(f32[1,4,4,1,128]{4,3,2,1,0:T(1,128)S(1)} %get-tuple-element.996), channel_id=1, source_target_pairs={{0,1},{1,2},{2,3},{4,5},{5,6},{6,7},{8,9},{9,10},{10,11},{12,13},{... | collective-permute-start | bytes 24584 | tf_op jit(solution)/shard_map/ppermute | solution.py:31
  270.7 12.3 %collective-permute-start.30 = (f32[3,1,2,2,128]{4,3,2,1,0:T(2,128)S(1)}, f32[3,1,2,2,128]{4,3,2,1,0:T(2,128)S(1)}, u32[]{:S(2)}, u32[]{:S(2)}) collective-permute-start(f32[3,1,2,2,128]{4,3,2,1,0:T(2,128)S(1)} %get-tuple-element.1013), channel_id=1, source_target_pairs={{0,16},{16,32},{32,48},{48,64},{64,80},{80,96},{96,112},{112,128},... | collective-permute-start | bytes 18440 | tf_op jit(solution)/shard_map/ppermute | solution.py:31
  274.6 8.4 %collective-permute-start.31 = (f32[3,1,2,2,128]{4,3,2,1,0:T(2,128)S(1)}, f32[3,1,2,2,128]{4,3,2,1,0:T(2,128)S(1)}, u32[]{:S(2)}, u32[]{:S(2)}) collective-permute-start(f32[3,1,2,2,128]{4,3,2,1,0:T(2,128)S(1)} %get-tuple-element.1014), channel_id=1, source_target_pairs={{16,0},{32,16},{48,32},{64,48},{80,64},{96,80},{112,96},{128,112},... | collective-permute-start | bytes 18440 | tf_op jit(solution)/shard_map/ppermute | solution.py:34
  279.2 0.7 copy-start.11
  283.1 5.9 %collective-permute-start.32 = (f32[3,4,1,2,128]{4,3,2,1,0:T(2,128)S(1)}, f32[3,4,1,2,128]{4,3,2,1,0:T(2,128)S(1)}, u32[]{:S(2)}, u32[]{:S(2)}) collective-permute-start(f32[3,4,1,2,128]{4,3,2,1,0:T(2,128)S(1)} %get-tuple-element.971), channel_id=1, source_target_pairs={{0,4},{4,8},{8,12},{1,5},{5,9},{9,13},{2,6},{6,10},{10,14},{3,7},{... | collective-permute-start | bytes 36872 | tf_op jit(solution)/shard_map/ppermute | solution.py:31
  285.3 5.6 %collective-permute-start.33 = (f32[3,4,1,2,128]{4,3,2,1,0:T(2,128)S(1)}, f32[3,4,1,2,128]{4,3,2,1,0:T(2,128)S(1)}, u32[]{:S(2)}, u32[]{:S(2)}) collective-permute-start(f32[3,4,1,2,128]{4,3,2,1,0:T(2,128)S(1)} %get-tuple-element.972), channel_id=1, source_target_pairs={{4,0},{8,4},{12,8},{5,1},{9,5},{13,9},{6,2},{10,6},{14,10},{7,3},{... | collective-permute-start | bytes 36872 | tf_op jit(solution)/shard_map/ppermute | solution.py:34
  291.0 15.1 %collective-permute-start.34 = (f32[3,4,4,1,128]{4,3,2,1,0:T(1,128)S(1)}, f32[3,4,4,1,128]{4,3,2,1,0:T(1,128)S(1)}, u32[]{:S(2)}, u32[]{:S(2)}) collective-permute-start(f32[3,4,4,1,128]{4,3,2,1,0:T(1,128)S(1)} %get-tuple-element.857), channel_id=1, source_target_pairs={{0,1},{1,2},{2,3},{4,5},{5,6},{6,7},{8,9},{9,10},{10,11},{12,13},{... | collective-permute-start | bytes 73736 | tf_op jit(solution)/shard_map/ppermute | solution.py:31
  292.9 13.1 %collective-permute-start.35 = (f32[3,4,4,1,128]{4,3,2,1,0:T(1,128)S(1)}, f32[3,4,4,1,128]{4,3,2,1,0:T(1,128)S(1)}, u32[]{:S(2)}, u32[]{:S(2)}) collective-permute-start(f32[3,4,4,1,128]{4,3,2,1,0:T(1,128)S(1)} %get-tuple-element.858), channel_id=1, source_target_pairs={{1,0},{2,1},{3,2},{5,4},{6,5},{7,6},{9,8},{10,9},{11,10},{13,12},{... | collective-permute-start | bytes 73736 | tf_op jit(solution)/shard_map/ppermute | solution.py:34
  355.9 25.3 %collective-permute-start.36 = (f32[1,1,2,2,128]{4,3,2,1,0:T(2,128)S(1)}, f32[1,1,2,2,128]{4,3,2,1,0:T(2,128)S(1)}, u32[]{:S(2)}, u32[]{:S(2)}) collective-permute-start(f32[1,1,2,2,128]{4,3,2,1,0:T(2,128)S(1)} %get-tuple-element.1049), channel_id=1, source_target_pairs={{0,16},{16,32},{32,48},{48,64},{64,80},{80,96},{96,112},{112,128},... | collective-permute-start | bytes 6152 | tf_op jit(solution)/shard_map/ppermute | solution.py:31
  358.7 22.5 %collective-permute-start.37 = (f32[1,1,2,2,128]{4,3,2,1,0:T(2,128)S(1)}, f32[1,1,2,2,128]{4,3,2,1,0:T(2,128)S(1)}, u32[]{:S(2)}, u32[]{:S(2)}) collective-permute-start(f32[1,1,2,2,128]{4,3,2,1,0:T(2,128)S(1)} %get-tuple-element.1050), channel_id=1, source_target_pairs={{16,0},{32,16},{48,32},{64,48},{80,64},{96,80},{112,96},{128,112},... | collective-permute-start | bytes 6152 | tf_op jit(solution)/shard_map/ppermute | solution.py:34
  381.2 4.4 %collective-permute-start.38 = (f32[1,4,1,2,128]{4,3,2,1,0:T(2,128)S(1)}, f32[1,4,1,2,128]{4,3,2,1,0:T(2,128)S(1)}, u32[]{:S(2)}, u32[]{:S(2)}) collective-permute-start(f32[1,4,1,2,128]{4,3,2,1,0:T(2,128)S(1)} %get-tuple-element.1037), channel_id=1, source_target_pairs={{0,4},{4,8},{8,12},{1,5},{5,9},{9,13},{2,6},{6,10},{10,14},{3,7},{... | collective-permute-start | bytes 12296 | tf_op jit(solution)/shard_map/ppermute | solution.py:31
  384.4 5.5 %collective-permute-start.39 = (f32[1,4,1,2,128]{4,3,2,1,0:T(2,128)S(1)}, f32[1,4,1,2,128]{4,3,2,1,0:T(2,128)S(1)}, u32[]{:S(2)}, u32[]{:S(2)}) collective-permute-start(f32[1,4,1,2,128]{4,3,2,1,0:T(2,128)S(1)} %get-tuple-element.1038), channel_id=1, source_target_pairs={{4,0},{8,4},{12,8},{5,1},{9,5},{13,9},{6,2},{10,6},{14,10},{7,3},{... | collective-permute-start | bytes 12296 | tf_op jit(solution)/shard_map/ppermute | solution.py:34
  389.9 4.4 %collective-permute-start.41 = (f32[1,4,4,1,128]{4,3,2,1,0:T(1,128)S(1)}, f32[1,4,4,1,128]{4,3,2,1,0:T(1,128)S(1)}, u32[]{:S(2)}, u32[]{:S(2)}) collective-permute-start(f32[1,4,4,1,128]{4,3,2,1,0:T(1,128)S(1)} %get-tuple-element.991), channel_id=1, source_target_pairs={{1,0},{2,1},{3,2},{5,4},{6,5},{7,6},{9,8},{10,9},{11,10},{13,12},{... | collective-permute-start | bytes 24584 | tf_op jit(solution)/shard_map/ppermute | solution.py:34
  391.8 6.5 %collective-permute-start.40 = (f32[1,4,4,1,128]{4,3,2,1,0:T(1,128)S(1)}, f32[1,4,4,1,128]{4,3,2,1,0:T(1,128)S(1)}, u32[]{:S(2)}, u32[]{:S(2)}) collective-permute-start(f32[1,4,4,1,128]{4,3,2,1,0:T(1,128)S(1)} %get-tuple-element.992), channel_id=1, source_target_pairs={{0,1},{1,2},{2,3},{4,5},{5,6},{6,7},{8,9},{9,10},{10,11},{12,13},{... | collective-permute-start | bytes 24584 | tf_op jit(solution)/shard_map/ppermute | solution.py:31
  (8 other events, 5.4 us)
